TPU v7x, 32 devices: a whole 2x2x4 slice. The times are simulated.
32 devices in a mesh: gx: 16 (over z, y, core), gy: 2 (over x).
Axes of the slice: x: 2, y: 2, z: 4, core: 2. Of those that a mesh axis runs over, the one named last changes fastest.
Arguments:
- grid_field: bfloat16 [2, 256, 64, 512], P(None, 'gx', 'gy'), may hold values from -6 to 6
- spectral_weight: bfloat16 [128, 2, 512, 512], P('gx', None, None, 'gy'), may hold values from -0.1875 to 0.1875
- skip_weight: bfloat16 [512, 512], replicated, may hold values from -0.25 to 0.25
- inner_weight: bfloat16 [1024, 512], replicated, may hold values from -0.25 to 0.25
- outer_weight: bfloat16 [1024, 512], replicated, may hold values from -0.1875 to 0.1875
Outputs:
- layer_out: bfloat16 [2, 256, 64, 512], P(None, 'gx', 'gy')
All inputs are finite; a program needn't handle non-finite values.
Results may differ from a plain program's by a relative error of at most 0.0093.
Values may be sent and summed in bfloat16 or wider, within the bound.
No kernel may reach another device: no remote copies, remote signals or barrier semaphores. Data moves between devices by JAX's collectives and lax.ppermute only.
A program may use at most 64 MiB of HBM per device.

v0:
```python
import math
import jax
import jax.numpy as jnp
from jax import lax
from jax.sharding import PartitionSpec as P

KX = 16
KY = 8


def phase_table(row_ids, col_ids, total_rows, total_cols):
    x_modes = jnp.arange(KX, dtype=jnp.int32)
    y_modes = jnp.arange(KY, dtype=jnp.int32)
    x_phase = (x_modes[:, None] * row_ids[None, :] % total_rows).astype(jnp.float32) / total_rows
    y_phase = (y_modes[:, None] * col_ids[None, :] % total_cols).astype(jnp.float32) / total_cols
    angles = (x_phase[:, None, :, None] + y_phase[None, :, None, :]) * (2.0 * math.pi)
    angles = angles.reshape(KX * KY, row_ids.shape[0] * col_ids.shape[0])
    return jnp.concatenate([jnp.cos(angles), -jnp.sin(angles)], axis=0).astype(jnp.bfloat16)


def local(grid_field, spectral_weight, skip_weight, inner_weight, outer_weight):
    micro_count, row_count, col_count, width_count = grid_field.shape
    x_devices = lax.axis_size("gx")
    y_devices = lax.axis_size("gy")
    total_rows = row_count * x_devices
    total_cols = col_count * y_devices
    mode_count = KX * KY
    row_ids = lax.axis_index("gx") * row_count + jnp.arange(row_count, dtype=jnp.int32)
    col_ids = lax.axis_index("gy") * col_count + jnp.arange(col_count, dtype=jnp.int32)
    basis = phase_table(row_ids, col_ids, total_rows, total_cols)
    flat_rows = grid_field.reshape(micro_count, row_count * col_count, width_count)
    partial_value = jnp.einsum("kn,bnc->kbc", basis, flat_rows, preferred_element_type=jnp.float32)
    partial_value = partial_value.reshape(2, mode_count, micro_count, width_count)
    owned_modes = lax.psum_scatter(partial_value, "gx", scatter_dimension=1, tiled=True)
    owned_modes = lax.psum(owned_modes, "gy")
    spectrum = (owned_modes * (1.0 / math.sqrt(total_rows * total_cols))).astype(jnp.bfloat16)
    weight_re = spectral_weight[:, 0]
    weight_im = spectral_weight[:, 1]
    mixed_re = jnp.einsum(
        "mbc,mcd->mbd", spectrum[0], weight_re, preferred_element_type=jnp.float32
    ) - jnp.einsum("mbc,mcd->mbd", spectrum[1], weight_im, preferred_element_type=jnp.float32)
    mixed_im = jnp.einsum(
        "mbc,mcd->mbd", spectrum[0], weight_im, preferred_element_type=jnp.float32
    ) + jnp.einsum("mbc,mcd->mbd", spectrum[1], weight_re, preferred_element_type=jnp.float32)
    mixed_modes = jnp.stack([mixed_re, mixed_im]).astype(jnp.bfloat16)
    gathered = lax.all_gather(mixed_modes, "gy", axis=3, tiled=True)
    gathered = lax.all_gather(gathered, "gx", axis=1, tiled=True)
    gathered = gathered.reshape(2 * mode_count, micro_count, width_count)
    spectral = jnp.einsum("kn,kbc->bnc", basis, gathered, preferred_element_type=jnp.float32)
    spectral = spectral * (1.0 / math.sqrt(mode_count))
    skip_term = jnp.einsum(
        "bnc,cd->bnd", flat_rows, skip_weight, preferred_element_type=jnp.float32
    )
    active = jax.nn.gelu(spectral + skip_term).astype(jnp.bfloat16)
    hidden = jax.nn.gelu(
        jnp.einsum("bnc,hc->bnh", active, inner_weight, preferred_element_type=jnp.float32)
    )
    hidden = hidden.astype(jnp.bfloat16)
    feed_forward = jnp.einsum(
        "bnh,hc->bnc", hidden, outer_weight, preferred_element_type=jnp.float32
    )
    layer_out = (active.astype(jnp.float32) + feed_forward).astype(jnp.bfloat16)
    return layer_out.reshape(micro_count, row_count, col_count, width_count)


def solution(mesh):
    in_specs = (P(None, "gx", "gy", None), P("gx", None, None, "gy"), P(), P(), P())
    out_specs = P(None, "gx", "gy", None)
    return jax.shard_map(local, mesh=mesh, in_specs=in_specs, out_specs=out_specs, check_vma=False)
```

profile of v0, /device:TPU:0, one launch (start us, length us, event | category | flops | bytes accessed | tf_op | source)
XLA Modules:
  0.0 143.6 jit_solution(16070263595739132689)
XLA Ops:
  6.5 0.0 copy-start
  6.5 0.0 reduce-scatter.2.cloned.1.call-start
  6.6 4.1 %cosine_convert_fusion = (bf16[16,8,16,32]{3,2,1,0:T(8,128)(2,1)S(1)}, bf16[16,8,16,32]{3,2,1,0:T(8,128)(2,1)S(1)}) fusion(f32[8,32]{1,0:T(8,128)S(1)} %fusion.65, f32[16,16]{1,0:T(8,128)S(1)} %fusion.59), kind=kLoop, calls=%fused_computation.41 | loop fusion | flops 327680 | bytes 264192 | tf_op jit(solution)/shard_map/convert.7
  10.7 0.4 cos.7
  11.2 0.1 copy.14
  11.3 0.5 neg.7
  11.8 0.1 copy.15
  11.9 0.1 copy.16
  12.1 0.0 copy-done
  12.1 1.4 fusion.73
  13.5 0.0 reduce-scatter.2.cloned.1.call-update
  13.5 0.0 all-reduce.2.cloned.1.call-start
  13.6 60.4 %reduce-scatter.2.cloned.1.call-done = f32[2,8,2,512]{3,1,2,0:T(8,128)} async-done(((f32[2,128,2,512]{3,1,2,0:T(8,128)}), f32[2,8,2,512]{3,1,2,0:T(8,128)}) %reduce-scatter.2.cloned.1.call-update) | async-done | bytes 65552 | tf_op jit(solution)/shard_map/reduce_scatter | solution.py:34
  74.0 0.0 all-reduce.2.cloned.1.call-update
  74.0 1.7 %fusion.49 = f32[2,512,512]{2,1,0:T(8,128)S(1)} fusion(bf16[2,512,512]{2,1,0:T(8,128)(2,1)S(1)} %bitcast.69, bf16[512,512]{1,0:T(8,128)(2,1)} %param.7), kind=kOutput, calls=%fused_computation.43 | convolution fusion | flops 536870912 | bytes 3670016 | tf_op jit(solution)/shard_map/bnc,cd->bnd/dot_general | solution.py:51
  75.7 20.5 %all-reduce.2.cloned.1.call-done = f32[2,8,2,512]{3,1,2,0:T(8,128)} async-done(((f32[2,8,2,512]{3,1,2,0:T(8,128)}), f32[2,8,2,512]{3,1,2,0:T(8,128)}) %all-reduce.2.cloned.1.call-update) | async-done | bytes 65552 | tf_op jit(solution)/shard_map/psum | solution.py:35
  96.2 0.8 multiply_convert_fusion
  97.1 0.0 copy-start.1
  97.1 2.1 %fusion.18 = f32[8,2,256]{2,1,0:T(2,128)S(1)} fusion(bf16[8,2,512,256]{3,2,1,0:T(8,128)(2,1)} %param.6, bf16[8,2,512]{2,0,1:T(8,128)(2,1)S(1)} %get-tuple-element.5), kind=kOutput, calls=%fused_computation.20 | convolution fusion | flops 4194304 | bytes 2129920 | tf_op jit(solution)/shard_map/mbc,mcd->mbd/dot_general | solution.py:41
  99.2 2.0 %fusion.16 = f32[8,2,256]{2,1,0:T(2,128)S(1)} fusion(bf16[8,2,512,256]{3,2,1,0:T(8,128)(2,1)} %param.6, bf16[8,2,512]{2,0,1:T(8,128)(2,1)S(1)} %get-tuple-element.6), kind=kOutput, calls=%fused_computation.18 | convolution fusion | flops 4194304 | bytes 2129920 | tf_op jit(solution)/shard_map/mbc,mcd->mbd/dot_general | solution.py:42
  101.2 0.0 copy-done.1
  101.2 0.4 fusion.40
  101.6 0.4 fusion.43
  102.0 4.4 %all_gather.6 = bf16[2,8,2,512]{3,2,1,0:T(2,128)(2,1)S(1)} all-gather(bf16[2,8,2,256]{3,2,1,0:T(2,128)(2,1)S(1)} %pad_maximum_fusion.1), channel_id=1, replica_groups=mesh['gx'=16,'gy'=2] {'gy'}, dimensions={3}, use_global_device_ids=true | all-gather | bytes 49152 | tf_op jit(solution)/shard_map/all_gather | solution.py:46
  106.4 22.9 %all_gather.7 = bf16[2,128,2,512]{3,2,1,0:T(2,128)(2,1)S(1)} all-gather(bf16[2,8,2,512]{3,2,1,0:T(2,128)(2,1)S(1)} %all_gather.6), channel_id=1, replica_groups=mesh['gx'=16,'gy'=2] {'gx'}, dimensions={1}, use_global_device_ids=true | all-gather | bytes 557056 | tf_op jit(solution)/shard_map/all_gather | solution.py:47
  129.3 1.9 %fusion.15 = bf16[2,512,512]{2,1,0:T(8,128)(2,1)} fusion(f32[2,512,512]{2,1,0:T(8,128)S(1)} %fusion.49, bf16[256,2,512]{2,1,0:T(2,128)(2,1)S(1)} %bitcast.72, bf16[128,512]{0,1:T(8,128)(2,1)S(1)} %copy.15, bf16[128,512]{0,1:T(8,128)(2,1)S(1)} %copy.14), kind=kOutput, calls=%fused_computation.17 | convolution fusion | flops 274726912 | bytes 3932160 | tf_op jit(solution)/shard_map/kn,kbc->bnc/dot_general | solution.py:49
  131.2 5.5 %add_convert_fusion = bf16[2,512,512]{2,1,0:T(8,128)(2,1)} fusion(bf16[2,512,512]{2,1,0:T(8,128)(2,1)} %fusion.15, bf16[1024,512]{1,0:T(8,128)(2,1)} %param.9, bf16[1024,512]{1,0:T(8,128)(2,1)} %param.8), kind=kOutput, calls=%fused_computation.27 | convolution fusion | flops 2158493696 | bytes 4194304 | tf_op jit(solution)/shard_map/bnh,hc->bnc/dot_general | solution.py:59
  (7 shorter events, 0.1 us)
Async XLA Ops:
  6.5 5.5 %copy-start = (bf16[2,16,32,512]{3,2,1,0:T(8,128)(2,1)S(1)}, bf16[2,16,32,512]{3,2,1,0:T(8,128)(2,1)}, u32[]{:S(2)}) copy-start(bf16[2,16,32,512]{3,2,1,0:T(8,128)(2,1)} %param.5) | copy-start | bytes 3145732
  6.5 67.4 %reduce-scatter.2.cloned.1.call-start = ((), (), s32[]{:S(2)}) async-start(), calls=%async_computation.1 | async-start | bytes 1114112 | tf_op jit(solution)/shard_map/reduce_scatter | solution.py:34
  13.5 82.7 %all-reduce.2.cloned.1.call-start = ((), (), s32[]{:S(2)}) async-start(), calls=%async_computation.2 | async-start | bytes 131072 | tf_op jit(solution)/shard_map/psum | solution.py:35
  97.1 4.1 %copy-start.1 = (bf16[8,2,512,256]{3,2,1,0:T(8,128)(2,1)S(1)}, bf16[8,2,512,256]{3,2,1,0:T(8,128)(2,1)}, u32[]{:S(2)}) copy-start(bf16[8,2,512,256]{3,2,1,0:T(8,128)(2,1)} %param.6) | copy-start | bytes 12582916
Sparse Core Ops, SparseCore 0:
  13.6 60.2 reduce-scatter.1
  76.2 20.0 all-reduce.1
where the time goes:
time: 144 us
  waiting for transfers between devices  80.9 us (56%)
  blocking collectives  27.3 us (19%)
  matrix products  15.5 us (11%)
  between operations  13.5 us (9%)
  other arithmetic  5.08 us (4%)
    reduce_scatter x1, waiting for transfers between devices, local(): lax.psum_scatter(partial_value, 'gx', scatter_dimension=1, tiled=True)  60.4 us
    all_gather x1, blocking collectives, local(): gathered = lax.all_gather(gathered, 'gx', axis=1, tiled=True)  22.9 us
    psum x1, waiting for transfers between devices, local(): owned_modes = lax.psum(owned_modes, 'gy')  20.5 us
    dot_general x1, matrix products, local(): jnp.einsum('bnh,hc->bnc', hidden, outer_weight, preferred_element_type=jn...  5.53 us
    all_gather x1, blocking collectives, local(): gathered = lax.all_gather(mixed_modes, 'gy', axis=3, tiled=True)  4.41 us
    another operation x1, other arithmetic  4.14 us
  transfers between devices with their start and end apart: 2, of which 2 were waited for; matrix products, arithmetic and copies ran while one was open for 1% of the time, Pallas kernels for 0%

commit v1 on v0

--- a/solution.py
+++ b/solution.py
@@ -32,7 +32,12 @@
     partial_value = jnp.einsum("kn,bnc->kbc", basis, flat_rows, preferred_element_type=jnp.float32)
     partial_value = partial_value.reshape(2, mode_count, micro_count, width_count)
     owned_modes = lax.psum_scatter(partial_value, "gx", scatter_dimension=1, tiled=True)
-    owned_modes = lax.psum(owned_modes, "gy")
+
+    def state_shape(obj):
+        near = jax.lax.all_gather(obj, axis_name="gy")
+        return jnp.sum(near, axis=0)
+
+    owned_modes = state_shape(owned_modes)
     spectrum = (owned_modes * (1.0 / math.sqrt(total_rows * total_cols))).astype(jnp.bfloat16)
     weight_re = spectral_weight[:, 0]
     weight_im = spectral_weight[:, 1]

time: 144 us -> 125 us (0.87)
  waiting for transfers between devices: 80.9 us -> 58.7 us
  blocking collectives: 27.3 us -> 30.4 us
    psum x1 -> x0, waiting for transfers between devices: 20.5 us -> none  [local(): owned_modes = lax.psum(owned_modes, 'gy')]
    all_gather x0 -> x1, blocking collectives: none -> 5.13 us  [state_shape(): near = jax.lax.all_gather(obj, axis_name='gy')]
    all_gather x1, blocking collectives: 22.9 us -> 20.8 us  [local(): gathered = lax.all_gather(gathered, 'gx', axis=1, tiled=True)]
    reduce_scatter x1, waiting for transfers between devices: 60.4 us -> 58.7 us  [local(): lax.psum_scatter(partial_value, 'gx', scatter_dimension=1, tiled=True)]
  transfers between devices with their start and end apart: 2 -> 1, of which waited for: 2 -> 1; matrix products, arithmetic and copies ran while one was open for 1% -> 1% of each run, Pallas kernels for 0% -> 0%
where the time goes in v1:
time: 125 us
  waiting for transfers between devices  58.7 us (47%)
  blocking collectives  30.4 us (24%)
  matrix products  15.5 us (12%)
  between operations  13.5 us (11%)
  other arithmetic  5.72 us (5%)
  local copies, waits for them, and re-layouts  1.29 us (1%)
    reduce_scatter x1, waiting for transfers between devices, local(): lax.psum_scatter(partial_value, 'gx', scatter_dimension=1, tiled=True)  58.7 us
    all_gather x1, blocking collectives, local(): gathered = lax.all_gather(gathered, 'gx', axis=1, tiled=True)  20.8 us
    dot_general x1, matrix products, local(): jnp.einsum('bnh,hc->bnc', hidden, outer_weight, preferred_element_type=jn...  5.53 us
    all_gather x1, blocking collectives, state_shape(): near = jax.lax.all_gather(obj, axis_name='gy')  5.13 us
    all_gather x1, blocking collectives, local(): gathered = lax.all_gather(mixed_modes, 'gy', axis=3, tiled=True)  4.41 us
    another operation x1, other arithmetic  4.14 us
  transfers between devices with their start and end apart: 1, of which 1 were waited for; matrix products, arithmetic and copies ran while one was open for 1% of the time, Pallas kernels for 0%

profile of v1, /device:TPU:0, one launch (start us, length us, event | category | flops | bytes accessed | tf_op | source)
XLA Modules:
  0.0 125.1 jit_solution(13347127083009650681)
XLA Ops:
  6.5 0.0 copy-start
  6.5 0.0 reduce-scatter.2.cloned.1.call-start
  6.6 4.1 %cosine_convert_fusion = (bf16[16,8,16,32]{3,2,1,0:T(8,128)(2,1)S(1)}, bf16[16,8,16,32]{3,2,1,0:T(8,128)(2,1)S(1)}) fusion(f32[8,32]{1,0:T(8,128)S(1)} %fusion.65, f32[16,16]{1,0:T(8,128)S(1)} %fusion.59), kind=kLoop, calls=%fused_computation.41 | loop fusion | flops 327680 | bytes 264192 | tf_op jit(solution)/shard_map/convert.7
  10.7 0.4 cos.7
  11.2 0.1 copy.23
  11.3 0.5 neg.7
  11.8 0.1 copy.24
  11.9 0.1 copy.25
  12.1 0.0 copy-done
  12.1 1.4 %fusion.73 = f32[2,128,2,512]{3,1,2,0:T(8,128)} fusion(bf16[2,128,512,1]{2,1,3,0:T(8,128)(2,1)S(1)} %bitcast.72, bf16[2,512,512,1]{2,1,0,3:T(8,128)(2,1)S(1)} %bitcast.71), kind=kOutput, calls=%fused_computation.80 | convolution fusion | flops 268435456 | bytes 2359296 | tf_op jit(solution)/shard_map/kn,bnc->kbc/dot_general | solution.py:32
  13.5 0.0 reduce-scatter.2.cloned.1.call-update
  13.5 1.7 %fusion.49 = f32[2,512,512]{2,1,0:T(8,128)S(1)} fusion(bf16[2,512,512]{2,1,0:T(8,128)(2,1)S(1)} %bitcast.70, bf16[512,512]{1,0:T(8,128)(2,1)} %param.7), kind=kOutput, calls=%fused_computation.43 | convolution fusion | flops 536870912 | bytes 3670016 | tf_op jit(solution)/shard_map/bnc,cd->bnd/dot_general | solution.py:56
  15.3 58.7 %reduce-scatter.2.cloned.1.call-done = f32[2,8,2,512]{3,1,2,0:T(8,128)} async-done(((f32[2,128,2,512]{3,1,2,0:T(8,128)}), f32[2,8,2,512]{3,1,2,0:T(8,128)}) %reduce-scatter.2.cloned.1.call-update) | async-done | bytes 65552 | tf_op jit(solution)/shard_map/reduce_scatter | solution.py:34
  74.0 5.1 %all-gather = f32[4,8,2,512]{3,1,2,0:T(8,128)S(1)} all-gather(f32[2,8,2,512]{3,1,2,0:T(8,128)} %reduce-scatter.2.cloned.1.call-done), channel_id=2, replica_groups=mesh['gx'=16,'gy'=2] {'gy'}, dimensions={0}, use_global_device_ids=true | all-gather | bytes 196608 | tf_op jit(solution)/shard_map/all_gather | solution.py:37
  79.1 0.6 reduce_sum.9
  79.7 0.8 multiply_convert_fusion
  80.6 0.0 copy-start.1
  80.6 2.1 %fusion.18 = f32[8,2,256]{2,1,0:T(2,128)S(1)} fusion(bf16[8,2,512,256]{3,2,1,0:T(8,128)(2,1)} %param.6, bf16[8,2,512]{2,0,1:T(8,128)(2,1)S(1)} %get-tuple-element.5), kind=kOutput, calls=%fused_computation.20 | convolution fusion | flops 4194304 | bytes 2129920 | tf_op jit(solution)/shard_map/mbc,mcd->mbd/dot_general | solution.py:46
  82.7 2.0 %fusion.16 = f32[8,2,256]{2,1,0:T(2,128)S(1)} fusion(bf16[8,2,512,256]{3,2,1,0:T(8,128)(2,1)} %param.6, bf16[8,2,512]{2,0,1:T(8,128)(2,1)S(1)} %get-tuple-element.6), kind=kOutput, calls=%fused_computation.18 | convolution fusion | flops 4194304 | bytes 2129920 | tf_op jit(solution)/shard_map/mbc,mcd->mbd/dot_general | solution.py:47
  84.7 0.0 copy-done.1
  84.7 0.4 fusion.40
  85.1 0.4 fusion.43
  85.5 4.4 %all_gather.14 = bf16[2,8,2,512]{3,2,1,0:T(2,128)(2,1)S(1)} all-gather(bf16[2,8,2,256]{3,2,1,0:T(2,128)(2,1)S(1)} %pad_maximum_fusion.1), channel_id=1, replica_groups=mesh['gx'=16,'gy'=2] {'gy'}, dimensions={3}, use_global_device_ids=true | all-gather | bytes 49152 | tf_op jit(solution)/shard_map/all_gather | solution.py:51
  89.9 20.8 %all_gather.15 = bf16[2,128,2,512]{3,2,1,0:T(2,128)(2,1)S(1)} all-gather(bf16[2,8,2,512]{3,2,1,0:T(2,128)(2,1)S(1)} %all_gather.14), channel_id=1, replica_groups=mesh['gx'=16,'gy'=2] {'gx'}, dimensions={1}, use_global_device_ids=true | all-gather | bytes 557056 | tf_op jit(solution)/shard_map/all_gather | solution.py:52
  110.8 1.9 %fusion.15 = bf16[2,512,512]{2,1,0:T(8,128)(2,1)} fusion(f32[2,512,512]{2,1,0:T(8,128)S(1)} %fusion.49, bf16[256,2,512]{2,1,0:T(2,128)(2,1)S(1)} %bitcast.74, bf16[128,512]{0,1:T(8,128)(2,1)S(1)} %copy.24, bf16[128,512]{0,1:T(8,128)(2,1)S(1)} %copy.23), kind=kOutput, calls=%fused_computation.17 | convolution fusion | flops 274726912 | bytes 3932160 | tf_op jit(solution)/shard_map/kn,kbc->bnc/dot_general | solution.py:54
  112.7 5.5 %add_convert_fusion = bf16[2,512,512]{2,1,0:T(8,128)(2,1)} fusion(bf16[2,512,512]{2,1,0:T(8,128)(2,1)} %fusion.15, bf16[1024,512]{1,0:T(8,128)(2,1)} %param.9, bf16[1024,512]{1,0:T(8,128)(2,1)} %param.8), kind=kOutput, calls=%fused_computation.27 | convolution fusion | flops 2158493696 | bytes 4194304 | tf_op jit(solution)/shard_map/bnh,hc->bnc/dot_general | solution.py:64
  (7 shorter events, 0.1 us)
Async XLA Ops:
  6.5 5.5 %copy-start = (bf16[2,16,32,512]{3,2,1,0:T(8,128)(2,1)S(1)}, bf16[2,16,32,512]{3,2,1,0:T(8,128)(2,1)}, u32[]{:S(2)}) copy-start(bf16[2,16,32,512]{3,2,1,0:T(8,128)(2,1)} %param.5) | copy-start | bytes 3145732
  6.5 67.4 %reduce-scatter.2.cloned.1.call-start = ((), (), s32[]{:S(2)}) async-start(), calls=%async_computation.1 | async-start | bytes 1114112 | tf_op jit(solution)/shard_map/reduce_scatter | solution.py:34
  80.6 4.1 %copy-start.1 = (bf16[8,2,512,256]{3,2,1,0:T(8,128)(2,1)S(1)}, bf16[8,2,512,256]{3,2,1,0:T(8,128)(2,1)}, u32[]{:S(2)}) copy-start(bf16[8,2,512,256]{3,2,1,0:T(8,128)(2,1)} %param.6) | copy-start | bytes 12582916
Sparse Core Ops, SparseCore 0:
  13.6 60.2 reduce-scatter.1

commit v2 on v0

--- a/solution.py
+++ b/solution.py
@@ -19,6 +19,11 @@
 
 
 def local(grid_field, spectral_weight, skip_weight, inner_weight, outer_weight):
+
+    def compute_keys(own_rows):
+        v_now = lax.all_gather(own_rows, "gx")
+        return jnp.concatenate(v_now, axis=1)
+
     micro_count, row_count, col_count, width_count = grid_field.shape
     x_devices = lax.axis_size("gx")
     y_devices = lax.axis_size("gy")
@@ -44,7 +49,7 @@
     ) + jnp.einsum("mbc,mcd->mbd", spectrum[1], weight_re, preferred_element_type=jnp.float32)
     mixed_modes = jnp.stack([mixed_re, mixed_im]).astype(jnp.bfloat16)
     gathered = lax.all_gather(mixed_modes, "gy", axis=3, tiled=True)
-    gathered = lax.all_gather(gathered, "gx", axis=1, tiled=True)
+    gathered = compute_keys(gathered)
     gathered = gathered.reshape(2 * mode_count, micro_count, width_count)
     spectral = jnp.einsum("kn,kbc->bnc", basis, gathered, preferred_element_type=jnp.float32)
     spectral = spectral * (1.0 / math.sqrt(mode_count))

time: 144 us -> 144 us (level)
  no operation moved by 1% of the time
where the time goes in v2:
time: 144 us
  waiting for transfers between devices  80.9 us (56%)
  blocking collectives  27.3 us (19%)
  matrix products  15.5 us (11%)
  between operations  13.5 us (9%)
  other arithmetic  5.08 us (4%)
    reduce_scatter x1, waiting for transfers between devices, local(): lax.psum_scatter(partial_value, 'gx', scatter_dimension=1, tiled=True)  60.4 us
    all_gather x1, blocking collectives, compute_keys(): v_now = lax.all_gather(own_rows, 'gx')  22.9 us
    psum x1, waiting for transfers between devices, local(): owned_modes = lax.psum(owned_modes, 'gy')  20.5 us
    dot_general x1, matrix products, local(): jnp.einsum('bnh,hc->bnc', hidden, outer_weight, preferred_element_type=jn...  5.53 us
    all_gather x1, blocking collectives, local(): gathered = lax.all_gather(mixed_modes, 'gy', axis=3, tiled=True)  4.41 us
    another operation x1, other arithmetic  4.14 us
  transfers between devices with their start and end apart: 2, of which 2 were waited for; matrix products, arithmetic and copies ran while one was open for 1% of the time, Pallas kernels for 0%

profile of v2, /device:TPU:0, one launch (start us, length us, event | category | flops | bytes accessed | tf_op | source)
XLA Modules:
  0.0 143.7 jit_solution(4513634466796870950)
XLA Ops:
  6.5 0.0 copy-start
  6.5 0.0 reduce-scatter.2.cloned.1.call-start
  6.6 4.1 %cosine_convert_fusion = (bf16[16,8,16,32]{3,2,1,0:T(8,128)(2,1)S(1)}, bf16[16,8,16,32]{3,2,1,0:T(8,128)(2,1)S(1)}) fusion(f32[8,32]{1,0:T(8,128)S(1)} %fusion.64, f32[16,16]{1,0:T(8,128)S(1)} %fusion.58), kind=kLoop, calls=%fused_computation.41 | loop fusion | flops 327680 | bytes 264192 | tf_op jit(solution)/shard_map/convert.7
  10.7 0.4 cos.7
  11.2 0.1 copy.24
  11.3 0.5 neg.7
  11.8 0.1 copy.25
  11.9 0.1 copy.26
  12.1 0.0 copy-done
  12.1 1.4 fusion.72
  13.5 0.0 reduce-scatter.2.cloned.1.call-update
  13.5 0.0 all-reduce.2.cloned.1.call-start
  13.6 60.4 %reduce-scatter.2.cloned.1.call-done = f32[2,8,2,512]{3,1,2,0:T(8,128)} async-done(((f32[2,128,2,512]{3,1,2,0:T(8,128)}), f32[2,8,2,512]{3,1,2,0:T(8,128)}) %reduce-scatter.2.cloned.1.call-update) | async-done | bytes 65552 | tf_op jit(solution)/shard_map/reduce_scatter | solution.py:39
  74.0 0.0 all-reduce.2.cloned.1.call-update
  74.0 1.7 %fusion.49 = f32[2,512,512]{2,1,0:T(8,128)S(1)} fusion(bf16[2,512,512]{2,1,0:T(8,128)(2,1)S(1)} %bitcast.73, bf16[512,512]{1,0:T(8,128)(2,1)} %param.7), kind=kOutput, calls=%fused_computation.43 | convolution fusion | flops 536870912 | bytes 3670016 | tf_op jit(solution)/shard_map/bnc,cd->bnd/dot_general | solution.py:56
  75.7 20.5 %all-reduce.2.cloned.1.call-done = f32[2,8,2,512]{3,1,2,0:T(8,128)} async-done(((f32[2,8,2,512]{3,1,2,0:T(8,128)}), f32[2,8,2,512]{3,1,2,0:T(8,128)}) %all-reduce.2.cloned.1.call-update) | async-done | bytes 65552 | tf_op jit(solution)/shard_map/psum | solution.py:40
  96.2 0.8 multiply_convert_fusion
  97.1 0.0 copy-start.1
  97.1 2.1 %fusion.18 = f32[8,2,256]{2,1,0:T(2,128)S(1)} fusion(bf16[8,2,512,256]{3,2,1,0:T(8,128)(2,1)} %param.6, bf16[8,2,512]{2,0,1:T(8,128)(2,1)S(1)} %get-tuple-element.5), kind=kOutput, calls=%fused_computation.20 | convolution fusion | flops 4194304 | bytes 2129920 | tf_op jit(solution)/shard_map/mbc,mcd->mbd/dot_general | solution.py:46
  99.2 2.0 %fusion.16 = f32[8,2,256]{2,1,0:T(2,128)S(1)} fusion(bf16[8,2,512,256]{3,2,1,0:T(8,128)(2,1)} %param.6, bf16[8,2,512]{2,0,1:T(8,128)(2,1)S(1)} %get-tuple-element.6), kind=kOutput, calls=%fused_computation.18 | convolution fusion | flops 4194304 | bytes 2129920 | tf_op jit(solution)/shard_map/mbc,mcd->mbd/dot_general | solution.py:47
  101.2 0.0 copy-done.1
  101.2 0.4 fusion.40
  101.6 0.4 fusion.43
  102.0 4.4 %all_gather.9 = bf16[2,8,2,512]{3,2,1,0:T(2,128)(2,1)S(1)} all-gather(bf16[2,8,2,256]{3,2,1,0:T(2,128)(2,1)S(1)} %pad_maximum_fusion.1), channel_id=1, replica_groups=mesh['gx'=16,'gy'=2] {'gy'}, dimensions={3}, use_global_device_ids=true | all-gather | bytes 49152 | tf_op jit(solution)/shard_map/all_gather | solution.py:51
  106.4 22.9 %all-gather = bf16[32,8,2,512]{3,1,2,0:T(8,128)(2,1)S(1)} all-gather(bf16[2,8,2,512]{3,1,2,0:T(8,128)(2,1)S(1)} %copy.33), channel_id=2, replica_groups=mesh['gx'=16,'gy'=2] {'gx'}, dimensions={0}, use_global_device_ids=true | all-gather | bytes 557056 | tf_op jit(solution)/shard_map/all_gather | solution.py:24
  129.4 1.9 %fusion.15 = bf16[2,512,512]{2,1,0:T(8,128)(2,1)} fusion(f32[2,512,512]{2,1,0:T(8,128)S(1)} %fusion.49, bf16[256,2,512]{2,0,1:T(8,128)(2,1)S(1)} %bitcast.77, bf16[128,512]{0,1:T(8,128)(2,1)S(1)} %copy.25, bf16[128,512]{0,1:T(8,128)(2,1)S(1)} %copy.24), kind=kOutput, calls=%fused_computation.17 | convolution fusion | flops 274726912 | bytes 3932160 | tf_op jit(solution)/shard_map/kn,kbc->bnc/dot_general | solution.py:54
  131.3 5.5 %add_convert_fusion = bf16[2,512,512]{2,1,0:T(8,128)(2,1)} fusion(bf16[2,512,512]{2,1,0:T(8,128)(2,1)} %fusion.15, bf16[1024,512]{1,0:T(8,128)(2,1)} %param.9, bf16[1024,512]{1,0:T(8,128)(2,1)} %param.8), kind=kOutput, calls=%fused_computation.27 | convolution fusion | flops 2158493696 | bytes 4194304 | tf_op jit(solution)/shard_map/bnh,hc->bnc/dot_general | solution.py:64
  (9 shorter events, 0.1 us)
Async XLA Ops:
  6.5 5.5 %copy-start = (bf16[2,16,32,512]{3,2,1,0:T(8,128)(2,1)S(1)}, bf16[2,16,32,512]{3,2,1,0:T(8,128)(2,1)}, u32[]{:S(2)}) copy-start(bf16[2,16,32,512]{3,2,1,0:T(8,128)(2,1)} %param.5) | copy-start | bytes 3145732
  6.5 67.4 %reduce-scatter.2.cloned.1.call-start = ((), (), s32[]{:S(2)}) async-start(), calls=%async_computation.1 | async-start | bytes 1114112 | tf_op jit(solution)/shard_map/reduce_scatter | solution.py:39
  13.5 82.7 %all-reduce.2.cloned.1.call-start = ((), (), s32[]{:S(2)}) async-start(), calls=%async_computation.2 | async-start | bytes 131072 | tf_op jit(solution)/shard_map/psum | solution.py:40
  97.1 4.1 %copy-start.1 = (bf16[8,2,512,256]{3,2,1,0:T(8,128)(2,1)S(1)}, bf16[8,2,512,256]{3,2,1,0:T(8,128)(2,1)}, u32[]{:S(2)}) copy-start(bf16[8,2,512,256]{3,2,1,0:T(8,128)(2,1)} %param.6) | copy-start | bytes 12582916
Sparse Core Ops, SparseCore 0:
  13.6 60.2 reduce-scatter.1
  76.2 20.0 all-reduce.1
